TPU v7x, 32 devices: a whole 2x2x4 slice. The times are simulated.
32 devices in a mesh: dp: 8 (over z, y), tensor: 4 (over x, core).
Axes of the slice: x: 2, y: 2, z: 4, core: 2. Of those that a mesh axis runs over, the one named last changes fastest.
Arguments:
- tokens: bfloat16 [16384, 4096], P('dp', 'tensor'), may hold values from -6 to 6
- cotangent: bfloat16 [16384, 1536], P('dp', 'tensor'), may hold values from -0.059814453 to 0.059814453
- seg_start: int32 [8, 2], P('dp'), may hold values from 0 to 1024, as said below
- seg_length: int32 [8, 2], P('dp'), may hold values from 0 to 1024, as said below
Outputs:
- weight_grad: float32 [4096, 2, 1536], P('dp', None, 'tensor')
Inputs may be any that keep to these rules, and one draw needn't show every extreme that they name: Within each index of dp the 2 segments lie in expert order, packed from row 0 without gaps: seg_start is the running sum of seg_length before each expert. `seg_length`: each length is at most 1024; in every draw some expert on some index of dp has exactly 1024 rows. Rows after the last segment belong to no expert.
All inputs are finite; a program needn't handle non-finite values.
Results may differ from a plain program's by a relative error of at most 0.0003.
Values may be sent and summed in bfloat16 or wider, within the bound.
No kernel may reach another device: no remote copies, remote signals or barrier semaphores. Data moves between devices by JAX's collectives and lax.ppermute only.
A program may use at most 128 MiB of HBM per device.

v0:
```python
import jax
import jax.numpy as jnp
from jax import lax
from jax.sharding import PartitionSpec as P

E_W = 2
CAP = 1024


def block_term(columns, grads, lower, upper, size):
    total_rows = columns.shape[0]
    first = jnp.minimum(lower, total_rows - size)
    rows = first + jnp.arange(size, dtype=jnp.int32)
    keep = (rows >= lower) & (rows < upper)
    block_x = lax.dynamic_slice_in_dim(columns, first, size, 0)
    block_g = lax.dynamic_slice_in_dim(grads, first, size, 0)
    block_g = jnp.where(keep[:, None], block_g, jnp.zeros_like(block_g))
    return lax.dot_general(
        block_x, block_g, (((0,), (0,)), ((), ())), preferred_element_type=jnp.float32
    )


def expert_term(columns, grads, start, length):
    return block_term(columns, grads, start, start + length, CAP)


def all_experts(columns, grads, seg_start, seg_length):
    terms = [
        expert_term(columns, grads, seg_start[0, expert], seg_length[0, expert])
        for expert in range(E_W)
    ]
    return jnp.stack(terms, 1)


def per_device(tokens, cotangent, seg_start, seg_length):
    whole = lax.all_gather(tokens, "tensor", axis=1, tiled=True)
    terms = all_experts(whole, cotangent, seg_start, seg_length)
    return lax.psum_scatter(terms, "dp", scatter_dimension=0, tiled=True)


def solution(mesh):
    in_specs = (P("dp", "tensor"), P("dp", "tensor"), P("dp", None), P("dp", None))
    out_specs = P("dp", None, "tensor")
    return jax.shard_map(
        per_device, mesh=mesh, in_specs=in_specs, out_specs=out_specs, check_vma=False
    )
```

profile of v0, /device:TPU:0, one launch (start us, length us, event | category | flops | bytes accessed | tf_op | source)
XLA Modules:
  0.0 359.4 jit_solution(8226653060245499362)
XLA Ops:
  6.5 0.0 all-gather.2.cloned.1.call-start
  6.5 0.7 all-gather.2.cloned.1.call-update
  7.3 0.0 reduce-scatter.2.cloned.1.call-start
  7.3 1.4 fusion.29
  10.0 1.3 fusion.28
  13.9 0.7 fusion.22
  14.5 0.7 fusion.23
  15.2 102.3 %all-gather.2.cloned.1.call-done = bf16[2048,4096]{1,0:T(8,128)(2,1)} async-done(((bf16[2048,1024]{1,0:T(8,128)(2,1)}), bf16[2048,4096]{1,0:T(8,128)(2,1)}) %all-gather.2.cloned.1.call-update) | async-done | bytes 16777232 | tf_op jit(solution)/shard_map/all_gather | solution.py:36
  117.5 0.0 copy-start
  117.5 0.0 copy-start.1
  117.5 7.5 %fusion.7 = f32[4096,1,384]{2,0,1:T(8,128)S(1)} fusion(bf16[2048,4096]{1,0:T(8,128)(2,1)} %all-gather.2.cloned.1.call-done, s32[]{:T(128)S(6)} %select_n.17, bf16[2048,384]{1,0:T(8,128)(2,1)} %param.5, pred[1024]{0:T(1024)(128)(4,1)S(1)} %fusion.23), kind=kOutput, calls=%fused_computation.6 | convolution fusion | flops 3221618688 | bytes 15468544 | tf_op jit(solution)/shard_map/dot_general | solution.py:18
  125.1 0.9 copy-done
  126.0 0.4 copy-done.1
  126.4 6.7 %fusion.4 = f32[4096,1,384]{2,0,1:T(8,128)} fusion(bf16[2048,4096]{1,0:T(8,128)(2,1)S(1)} %copy-done, s32[]{:T(128)S(6)} %select_n.15, bf16[2048,384]{1,0:T(8,128)(2,1)S(1)} %copy-done.1, pred[1024]{0:T(1024)(128)(4,1)S(1)} %fusion.22), kind=kOutput, calls=%fused_computation.5 | convolution fusion | flops 3221618688 | bytes 15468544 | tf_op jit(solution)/shard_map/dot_general | solution.py:18
  133.1 8.1 %pad_maximum_fusion = f32[4096,2,384]{2,0,1:T(8,128)} fusion(f32[4096,1,384]{2,0,1:T(8,128)S(1)} %fusion.7, f32[4096,1,384]{2,0,1:T(8,128)} %fusion.4), kind=kLoop, calls=%fused_computation | loop fusion | flops 3145728 | bytes 25165824 | tf_op jit(solution)/shard_map/stack | solution.py:32
  141.2 0.0 reduce-scatter.2.cloned.1.call-update
  141.2 207.6 %reduce-scatter.2.cloned.1.call-done = f32[512,2,384]{2,0,1:T(8,128)} async-done(((f32[4096,2,384]{2,0,1:T(8,128)}), f32[512,2,384]{2,0,1:T(8,128)}) %reduce-scatter.2.cloned.1.call-update) | async-done | bytes 1572880 | tf_op jit(solution)/shard_map/reduce_scatter | solution.py:38
  348.8 3.8 %copy.5 = f32[512,2,384]{2,1,0:T(2,128)} copy(f32[512,2,384]{2,0,1:T(8,128)} %reduce-scatter.2.cloned.1.call-done) | data formatting | bytes 3145728 | tf_op jit(solution)/shard_map/reduce_scatter | solution.py:38
Async XLA Ops:
  6.5 111.0 %all-gather.2.cloned.1.call-start = ((), (), s32[]{:S(2)}) async-start(), calls=%async_computation.1 | async-start | bytes 20971520 | tf_op jit(solution)/shard_map/all_gather | solution.py:36
  7.3 341.6 %reduce-scatter.2.cloned.1.call-start = ((), (), s32[]{:S(2)}) async-start(), calls=%async_computation.2 | async-start | bytes 14155776 | tf_op jit(solution)/shard_map/reduce_scatter | solution.py:38
  117.5 8.5 %copy-start = (bf16[2048,4096]{1,0:T(8,128)(2,1)S(1)}, bf16[2048,4096]{1,0:T(8,128)(2,1)}, u32[]{:S(2)}) copy-start(bf16[2048,4096]{1,0:T(8,128)(2,1)} %all-gather.2.cloned.1.call-done) | copy-start | bytes 50331652
  117.5 8.9 %copy-start.1 = (bf16[2048,384]{1,0:T(8,128)(2,1)S(1)}, bf16[2048,384]{1,0:T(8,128)(2,1)}, u32[]{:S(2)}) copy-start(bf16[2048,384]{1,0:T(8,128)(2,1)} %param.5) | copy-start | bytes 4718596
Sparse Core Ops, SparseCore 0:
  8.9 108.6 all-gather.1
  141.4 207.4 reduce-scatter.1
where the time goes:
time: 360 us; the launch traced here: 359 us
  waiting for transfers between devices  311 us (86%)
  between operations  17.3 us (5%)
  matrix products  14.2 us (4%)
  other arithmetic  9.47 us (3%)
  local copies, waits for them, and re-layouts  7.8 us (2%)
    reduce_scatter x1, waiting for transfers between devices, per_device(): return lax.psum_scatter(terms, 'dp', scatter_dimension=0, tiled=True)  208 us
    all_gather x1, waiting for transfers between devices, per_device(): whole = lax.all_gather(tokens, 'tensor', axis=1, tiled=True)  102 us
    dot_general x2, matrix products, block_term(): lax.dot_general(block_x, block_g, (((0,), (0,)), ((), ())), preferred_ele...  14.2 us
    another operation x1, other arithmetic, all_experts(): return jnp.stack(terms, 1)  8.12 us
  transfers between devices with their start and end apart: 2, of which 2 were waited for; matrix products, arithmetic and copies ran while one was open for 1% of the time, Pallas kernels for 0%

commit v1 on v0

v1 whole, which is shorter than its diff:
```python
import jax
import jax.numpy as jnp
from jax import lax
from jax.sharding import PartitionSpec as P

CHUNKS = 4
TOP = 15.0
TAIL = 16
HALF = True


def swap(n, bit):
    return [(i, i ^ bit) for i in range(n)]


def coded_pieces(pieces):
    peak = jnp.max(jnp.abs(jnp.stack(pieces)))
    power = jnp.ceil(jnp.log2(jnp.maximum(peak, 1e-30))) + 1.0
    tail = jnp.full((TAIL, pieces[0].shape[1]), power, jnp.float32)
    scale = jnp.exp2(TOP - power)
    return [jnp.concatenate([p * scale, tail], 0).astype(jnp.float16) for p in pieces]


def decoded(coded):
    coded = coded.astype(jnp.float32)
    return coded[:-TAIL] * jnp.exp2(coded[-1:] - TOP)


def spread(block, n_tensor):
    got = {0: block}
    bit = n_tensor // 2
    while bit:
        for k, value in list(got.items()):
            got[k ^ bit] = lax.ppermute(value, "tensor", swap(n_tensor, bit))
        bit //= 2
    return got


def solution(mesh):
    n_dp, n_tensor = mesh.shape["dp"], mesh.shape["tensor"]
    pair = swap(n_dp, 1)
    outer = n_dp // 2
    groups = [[2 * o + i for o in range(outer)] for i in range(2)]

    def per_device(tokens, cotangent, seg_start, seg_length):
        experts = seg_start.shape[1]
        assert experts == 2
        cap = tokens.shape[0] // experts
        width = tokens.shape[1]
        hidden = cotangent.shape[1]
        mine = lax.axis_index("dp") % 2
        here = lax.axis_index("tensor")
        pieces = max(outer // n_tensor, 1)
        part = width // (pieces * 2 * CHUNKS)

        def bounds(expert):
            start = lax.dynamic_index_in_dim(seg_start[0], expert, 0, False)
            length = lax.dynamic_index_in_dim(seg_length[0], expert, 0, False)
            return jnp.minimum(start, tokens.shape[0] - cap), start, start + length

        def columns(expert, c):
            first = bounds(expert)[0]
            step = width // (2 * pieces)
            cols = [
                lax.dynamic_slice(tokens, (first, j * step + c * part), (cap, part))
                for j in range(2 * pieces)
            ]
            return jnp.concatenate(cols, 1)

        def grads(expert):
            first, start, end = bounds(expert)
            rows = first + jnp.arange(cap, dtype=jnp.int32)
            keep = (rows >= start) & (rows < end)
            g = lax.dynamic_slice_in_dim(cotangent, first, cap, 0)
            return jnp.where(keep[:, None], g, jnp.zeros_like(g))

        x_in = []
        for c in range(CHUNKS):
            x_in.append(lax.ppermute(columns(1 - mine, c), "dp", pair))
        g_own = grads(mine)
        g_in = lax.ppermute(grads(1 - mine), "dp", pair)
        g = jnp.concatenate([g_own, g_in], 0)
        kept, sent = [], []
        for c in range(CHUNKS):
            got = spread(jnp.concatenate([columns(mine, c), x_in[c]], 0), n_tensor)
            dims = (((0,), (0,)), ((), ()))
            terms = [
                lax.dot_general(got[k], g, dims, preferred_element_type=jnp.float32)
                for k in range(n_tensor)
            ]
            if HALF and outer == n_tensor:
                stacked = jnp.stack(terms)
                away = (lax.axis_index("dp") // 2) ^ here
                split = [
                    lax.dynamic_index_in_dim(stacked, away ^ d, 0, False) for d in range(outer)
                ]
                coded = coded_pieces(split[1:])
                piece = split[0]
                for d in range(1, outer):
                    moved = lax.ppermute(coded[d - 1], "dp", swap(n_dp, 2 * d))
                    piece += decoded(moved)
            else:
                total = jnp.zeros((n_tensor,) + terms[0].shape, jnp.float32)
                for k in range(n_tensor):
                    total = lax.dynamic_update_index_in_dim(total, terms[k], here ^ k, 0)
                total = total.reshape(outer, -1, hidden)
                piece = lax.psum_scatter(
                    total, "dp", scatter_dimension=0, axis_index_groups=groups, tiled=True
                )
            piece = piece.reshape(2, part, hidden)
            kept.append(lax.dynamic_index_in_dim(piece, mine, 0, False))
            out = lax.dynamic_index_in_dim(piece, 1 - mine, 0, False)
            sent.append(lax.ppermute(out, "dp", pair))
        kept = jnp.concatenate(kept, 0)
        sent = jnp.concatenate(sent, 0)
        first = jnp.where(mine == 0, kept, sent)
        second = jnp.where(mine == 0, sent, kept)
        return jnp.stack([first, second], 1)

    in_specs = (P("dp", "tensor"), P("dp", "tensor"), P("dp", None), P("dp", None))
    out_specs = P("dp", None, "tensor")

    return jax.shard_map(
        per_device, mesh=mesh, in_specs=in_specs, out_specs=out_specs, check_vma=False
    )
```

time: 360 us -> 276 us (0.77)
  waiting for transfers between devices: 311 us -> 131 us
  starting transfers between devices: 0.04 us -> 49.8 us
  matrix products: 14.2 us -> 38.6 us
  other arithmetic: 9.47 us -> 29.1 us
  between operations: 17.3 us -> 7.71 us
  local copies, waits for them, and re-layouts: 7.8 us -> 16.3 us
    reduce_scatter x1 -> x0, waiting for transfers between devices: 208 us -> none  [per_device(): return lax.psum_scatter(terms, 'dp', scatter_dimension=0, tiled=True)]
    ppermute x0 -> x33, waiting for transfers between devices: none -> 131 us  [the longest x4 47.2 us: per_device(): x_in.append(lax.ppermute(columns(1 - mine, c), 'dp', pair))]
    all_gather x1 -> x0, waiting for transfers between devices: 102 us -> none  [per_device(): whole = lax.all_gather(tokens, 'tensor', axis=1, tiled=True)]
    ppermute x0 -> x33, starting transfers between devices: none -> 49.8 us  [the longest x12 31.2 us: per_device(): moved = lax.ppermute(coded[d - 1], 'dp', swap(n_dp, 2 * d))]
    dot_general x2 -> x16, matrix products: 14.2 us -> 38.6 us  [per_device(): lax.dot_general(got[k], g, dims, preferred_element_type=jnp.float32)]
    mul x0 -> x12, other arithmetic: none -> 13.8 us  [coded_pieces(): p * scale]
    another operation x1 -> x5, other arithmetic: 8.12 us -> 0.52 us  [the longest x4 0.42 us: per_device(): stacked = jnp.stack(terms)]
    dynamic_slice x0 -> x6, local copies, waits for them, and re-layouts: none -> 7.24 us  [the longest x1 4.52 us: columns(): lax.dynamic_slice(tokens, (first, j * step + c * part), (cap, part))]
  transfers between devices with their start and end apart: 2 -> 33, of which waited for: 2 -> 11; matrix products, arithmetic and copies ran while one was open for 1% -> 23% of each run, Pallas kernels for 0% -> 0%
where the time goes in v1:
time: 276 us; the launch traced here: 273 us
  waiting for transfers between devices  131 us (47%)
  starting transfers between devices  49.8 us (18%)
  matrix products  38.6 us (14%)
  other arithmetic  29.1 us (11%)
  local copies, waits for them, and re-layouts  16.3 us (6%)
  between operations  7.71 us (3%)
    ppermute x4, waiting for transfers between devices, per_device(): x_in.append(lax.ppermute(columns(1 - mine, c), 'dp', pair))  47.2 us
    ppermute x12, waiting for transfers between devices, spread(): got[k ^ bit] = lax.ppermute(value, 'tensor', swap(n_tensor, bit))  41.7 us
    dot_general x16, matrix products, per_device(): lax.dot_general(got[k], g, dims, preferred_element_type=jnp.float32)  38.6 us
    ppermute x12, waiting for transfers between devices, per_device(): moved = lax.ppermute(coded[d - 1], 'dp', swap(n_dp, 2 * d))  35.8 us
    ppermute x12, starting transfers between devices, per_device(): moved = lax.ppermute(coded[d - 1], 'dp', swap(n_dp, 2 * d))  31.2 us
    mul x12, other arithmetic, coded_pieces(): p * scale  13.8 us
    ppermute x12, starting transfers between devices, spread(): got[k ^ bit] = lax.ppermute(value, 'tensor', swap(n_tensor, bit))  7.12 us
    ppermute x4, waiting for transfers between devices, per_device(): sent.append(lax.ppermute(out, 'dp', pair))  6.57 us
  transfers between devices with their start and end apart: 33, of which 11 were waited for; matrix products, arithmetic and copies ran while one was open for 23% of the time, Pallas kernels for 0%

profile of v1, /device:TPU:0, one launch (start us, length us, event | category | flops | bytes accessed | tf_op | source)
XLA Modules:
  0.0 272.7 jit_solution(3719307152300266181)
XLA Ops:
  2.8 4.5 %constant_dynamic-slice_fusion.16 = (bf16[1024,128]{1,0:T(8,128)(2,1)}, bf16[1024,128]{1,0:T(8,128)(2,1)}, bf16[1024,128]{1,0:T(8,128)(2,1)}, bf16[1024,128]{1,0...) fusion(bf16[2048,1024]{1,0:T(8,128)(2,1)} %param.4, ...), kind=kLoop, calls=%fused_computation.116 | loop fusion | bytes 8388616 | tf_op jit(solution)/shard_map/dynamic_slice | solution.py:65
  8.2 3.0 %collective-permute-start.8 = (bf16[1024,256]{1,0:T(8,128)(2,1)}, bf16[1024,256]{1,0:T(8,128)(2,1)}, u32[]{:S(2)}, u32[]{:S(2)}) collective-permute-start(bf16[1024,256]{1,0:T(8,128)(2,1)} %pad_maximum_fusion.13), channel_id=1, source_target_pairs={{0,4},{4,0},{8,12},{12,8},{16,20},{20,16},{24,28},{28,24},{1,5},{5... | collective-permute-start | bytes 1572872 | tf_op jit(solution)/shard_map/ppermute | solution.py:79
  20.0 2.1 collective-permute-start
  22.1 13.4 %collective-permute-done.15 = bf16[1024,256]{1,0:T(8,128)(2,1)} collective-permute-done((bf16[1024,256]{1,0:T(8,128)(2,1)}, bf16[1024,256]{1,0:T(8,128)(2,1)}, u32[]{:S(2)}, u32[]{:S(2)}) %collective-permute-start.15) | collective-permute-done | bytes 524320 | tf_op jit(solution)/shard_map/ppermute | solution.py:79
  36.7 2.1 collective-permute-start.17
  39.9 23.5 %collective-permute-done.22 = bf16[1024,256]{1,0:T(8,128)(2,1)S(1)} collective-permute-done((bf16[1024,256]{1,0:T(8,128)(2,1)S(1)}, bf16[1024,256]{1,0:T(8,128)(2,1)S(1)}, u32[]{:S(2)}, u32[]{:S(2)}) %collective-permute-start.22) | collective-permute-done | bytes 524320 | tf_op jit(solution)/shard_map/ppermute | solution.py:79
  63.6 10.3 %collective-permute-done = bf16[1024,256]{1,0:T(8,128)(2,1)S(1)} collective-permute-done((bf16[1024,256]{1,0:T(8,128)(2,1)S(1)}, bf16[1024,256]{1,0:T(8,128)(2,1)S(1)}, u32[]{:S(2)}, u32[]{:S(2)}) %collective-permute-start) | collective-permute-done | bytes 524320 | tf_op jit(solution)/shard_map/ppermute | solution.py:79
  77.9 2.6 convolution_bitcast_fusion.15
  80.6 2.8 %convolution_bitcast_fusion.11 = f32[1,256,384]{2,1,0:T(8,128)} fusion(bf16[1024,256]{1,0:T(8,128)(2,1)} %collective-permute-done.8, bf16[1024,128]{1,0:T(8,128)(2,1)S(1)} %get-tuple-element.14, bf16[1024,128]{1,0:T(8,128)(2,1)S(1)} %copy-done.11, bf16[1024,384]{1,0:T(8,128)(2,1)} %collective-permute-done.1, bf16[1024,384]{1,0:T(8,128)(2,1)S(1)} %copy-done.24), kind=kOutput, calls=%fused_computation.17 | convolution fusion | flops 408944640 | bytes 3014656 | tf_op jit(solution)/shard_map/dot_general | solution.py:88
  83.4 2.8 %convolution_bitcast_fusion.7 = f32[1,256,384]{2,1,0:T(8,128)} fusion(bf16[1024,256]{1,0:T(8,128)(2,1)} %collective-permute-done.15, bf16[1024,128]{1,0:T(8,128)(2,1)S(1)} %get-tuple-element.10, bf16[1024,128]{1,0:T(8,128)(2,1)S(1)} %get-tuple-element.11, bf16[1024,384]{1,0:T(8,128)(2,1)} %collective-permute-done.1, bf16[1024,384]{1,0:T(8,128)(2,1)S(1)} %copy-done.24), kind=kOutput, calls=%fused_computation.13 | convolution fusion | flops 408944640 | bytes 3014656 | tf_op jit(solution)/shard_map/dot_general | solution.py:88
  87.9 2.6 convolution_bitcast_fusion.6
  90.6 3.0 %convolution_bitcast_fusion.5 = f32[1,256,384]{2,1,0:T(8,128)} fusion(bf16[2048,256]{1,0:T(8,128)(2,1)} %collective-permute-done.17, bf16[1024,384]{1,0:T(8,128)(2,1)} %collective-permute-done.1, bf16[1024,384]{1,0:T(8,128)(2,1)S(1)} %copy-done.24), kind=kOutput, calls=%fused_computation.11 | convolution fusion | flops 405798912 | bytes 3014656 | tf_op jit(solution)/shard_map/dot_general | solution.py:88
  93.5 28.8 %collective-permute-done.24 = bf16[2048,256]{1,0:T(8,128)(2,1)S(1)} collective-permute-done((bf16[2048,256]{1,0:T(8,128)(2,1)S(1)}, bf16[2048,256]{1,0:T(8,128)(2,1)S(1)}, u32[]{:S(2)}, u32[]{:S(2)}) %collective-permute-start.24) | collective-permute-done | bytes 1048608 | tf_op jit(solution)/shard_map/ppermute | solution.py:34
  124.8 2.6 convolution_bitcast_fusion.10
  127.5 2.9 %convolution_bitcast_fusion.9 = f32[1,256,384]{2,1,0:T(8,128)} fusion(bf16[2048,256]{1,0:T(8,128)(2,1)} %collective-permute-done.10, bf16[1024,384]{1,0:T(8,128)(2,1)} %collective-permute-done.1, bf16[1024,384]{1,0:T(8,128)(2,1)S(1)} %copy-done.24), kind=kOutput, calls=%fused_computation.15 | convolution fusion | flops 405798912 | bytes 3014656 | tf_op jit(solution)/shard_map/dot_general | solution.py:88
  130.4 12.8 %collective-permute-done.3 = bf16[2048,256]{1,0:T(8,128)(2,1)} collective-permute-done((bf16[2048,256]{1,0:T(8,128)(2,1)S(1)}, bf16[2048,256]{1,0:T(8,128)(2,1)}, u32[]{:S(2)}, u32[]{:S(2)}) %collective-permute-start.3) | collective-permute-done | bytes 1048608 | tf_op jit(solution)/shard_map/ppermute | solution.py:34
  143.2 2.2 convolution_bitcast_fusion.13
  146.0 2.6 convolution_bitcast_fusion.14
  155.5 2.3 convolution_bitcast_fusion.12
  166.5 2.3 convolution_bitcast_fusion.8
  178.7 2.3 convolution_bitcast_fusion.4
  188.2 2.6 collective-permute-start.27
  192.5 2.9 %collective-permute-start.6 = (f16[272,384]{1,0:T(8,128)(2,1)S(1)}, f16[272,384]{1,0:T(8,128)(2,1)S(1)}, u32[]{:S(2)}, u32[]{:S(2)}) collective-permute-start(f16[272,384]{1,0:T(8,128)(2,1)S(1)} %concatenate.130), channel_id=1, source_target_pairs={{0,16},{4,20},{8,24},{12,28},{16,0},{20,4},{24,8},{28,12},{1,17},{... | collective-permute-start | bytes 626696 | tf_op jit(solution)/shard_map/ppermute | solution.py:100
  197.1 10.0 %collective-permute-done.27 = f16[272,384]{1,0:T(8,128)(2,1)S(1)} collective-permute-done((f16[272,384]{1,0:T(8,128)(2,1)S(1)}, f16[272,384]{1,0:T(8,128)(2,1)S(1)}, u32[]{:S(2)}, u32[]{:S(2)}) %collective-permute-start.27) | collective-permute-done | bytes 208928 | tf_op jit(solution)/shard_map/ppermute | solution.py:100
  207.1 14.2 %collective-permute-start.13 = (f16[272,384]{1,0:T(8,128)(2,1)S(1)}, f16[272,384]{1,0:T(8,128)(2,1)S(1)}, u32[]{:S(2)}, u32[]{:S(2)}) collective-permute-start(f16[272,384]{1,0:T(8,128)(2,1)S(1)} %concatenate.137), channel_id=1, source_target_pairs={{0,16},{4,20},{8,24},{12,28},{16,0},{20,4},{24,8},{28,12},{1,17},{... | collective-permute-start | bytes 626696 | tf_op jit(solution)/shard_map/ppermute | solution.py:100
  222.7 10.3 %collective-permute-done.6 = f16[272,384]{1,0:T(8,128)(2,1)S(1)} collective-permute-done((f16[272,384]{1,0:T(8,128)(2,1)S(1)}, f16[272,384]{1,0:T(8,128)(2,1)S(1)}, u32[]{:S(2)}, u32[]{:S(2)}) %collective-permute-start.6) | collective-permute-done | bytes 208928 | tf_op jit(solution)/shard_map/ppermute | solution.py:100
  233.1 6.0 %collective-permute-start.20 = (f16[272,384]{1,0:T(8,128)(2,1)S(1)}, f16[272,384]{1,0:T(8,128)(2,1)S(1)}, u32[]{:S(2)}, u32[]{:S(2)}) collective-permute-start(f16[272,384]{1,0:T(8,128)(2,1)S(1)} %concatenate.144), channel_id=1, source_target_pairs={{0,16},{4,20},{8,24},{12,28},{16,0},{20,4},{24,8},{28,12},{1,17},{... | collective-permute-start | bytes 626696 | tf_op jit(solution)/shard_map/ppermute | solution.py:100
  240.8 10.2 %collective-permute-done.13 = f16[272,384]{1,0:T(8,128)(2,1)S(1)} collective-permute-done((f16[272,384]{1,0:T(8,128)(2,1)S(1)}, f16[272,384]{1,0:T(8,128)(2,1)S(1)}, u32[]{:S(2)}, u32[]{:S(2)}) %collective-permute-start.13) | collective-permute-done | bytes 208928 | tf_op jit(solution)/shard_map/ppermute | solution.py:100
  254.6 5.3 %collective-permute-done.20 = f16[272,384]{1,0:T(8,128)(2,1)S(1)} collective-permute-done((f16[272,384]{1,0:T(8,128)(2,1)S(1)}, f16[272,384]{1,0:T(8,128)(2,1)S(1)}, u32[]{:S(2)}, u32[]{:S(2)}) %collective-permute-start.20) | collective-permute-done | bytes 208928 | tf_op jit(solution)/shard_map/ppermute | solution.py:100
  263.5 4.2 %collective-permute-done.30 = f32[128,384]{1,0:T(8,128)S(1)} collective-permute-done((f32[128,384]{1,0:T(8,128)S(1)}, f32[128,384]{1,0:T(8,128)S(1)}, u32[]{:S(2)}, u32[]{:S(2)}) %collective-permute-start.30) | collective-permute-done | bytes 196640 | tf_op jit(solution)/shard_map/ppermute | solution.py:113
  267.7 2.3 collective-permute-done.31
  270.4 2.4 copy.5
  (206 shorter events, 63.1 us)
Async XLA Ops:
  8.2 28.6 %collective-permute-start.8 = (bf16[1024,256]{1,0:T(8,128)(2,1)}, bf16[1024,256]{1,0:T(8,128)(2,1)}, u32[]{:S(2)}, u32[]{:S(2)}) collective-permute-start(bf16[1024,256]{1,0:T(8,128)(2,1)} %pad_maximum_fusion.13), channel_id=1, source_target_pairs={{0,4},{4,0},{8,12},{12,8},{16,20},{20,16},{24,28},{28,24},{1,5},{5... | collective-permute-start | bytes 1572872 | tf_op jit(solution)/shard_map/ppermute | solution.py:79
  12.0 23.4 %collective-permute-start.15 = (bf16[1024,256]{1,0:T(8,128)(2,1)}, bf16[1024,256]{1,0:T(8,128)(2,1)}, u32[]{:S(2)}, u32[]{:S(2)}) collective-permute-start(bf16[1024,256]{1,0:T(8,128)(2,1)} %pad_maximum_fusion.14), channel_id=1, source_target_pairs={{0,4},{4,0},{8,12},{12,8},{16,20},{20,16},{24,28},{28,24},{1,5},{5... | collective-permute-start | bytes 1572872 | tf_op jit(solution)/shard_map/ppermute | solution.py:79
  17.8 57.9 %collective-permute-start.1 = (bf16[1024,384]{1,0:T(8,128)(2,1)}, bf16[1024,384]{1,0:T(8,128)(2,1)}, u32[]{:S(2)}, u32[]{:S(2)}) collective-permute-start(bf16[1024,384]{1,0:T(8,128)(2,1)} %get-tuple-element.36), channel_id=1, source_target_pairs={{0,4},{4,0},{8,12},{12,8},{16,20},{20,16},{24,28},{28,24},{1,5},{5... | collective-permute-start | bytes 2359304 | tf_op jit(solution)/shard_map/ppermute | solution.py:81
  19.9 43.6 %collective-permute-start.22 = (bf16[1024,256]{1,0:T(8,128)(2,1)S(1)}, bf16[1024,256]{1,0:T(8,128)(2,1)S(1)}, u32[]{:S(2)}, u32[]{:S(2)}) collective-permute-start(bf16[1024,256]{1,0:T(8,128)(2,1)S(1)} %pad_maximum_fusion.15), channel_id=1, source_target_pairs={{0,4},{4,0},{8,12},{12,8},{16,20},{20,16},{24,28},{28,24},{1,5},{5... | collective-permute-start | bytes 1572872 | tf_op jit(solution)/shard_map/ppermute | solution.py:79
  20.0 53.8 %collective-permute-start = (bf16[1024,256]{1,0:T(8,128)(2,1)S(1)}, bf16[1024,256]{1,0:T(8,128)(2,1)S(1)}, u32[]{:S(2)}, u32[]{:S(2)}) collective-permute-start(bf16[1024,256]{1,0:T(8,128)(2,1)S(1)} %pad_maximum_fusion.12), channel_id=1, source_target_pairs={{0,4},{4,0},{8,12},{12,8},{16,20},{20,16},{24,28},{28,24},{1,5},{5... | collective-permute-start | bytes 1572872 | tf_op jit(solution)/shard_map/ppermute | solution.py:79
  36.6 49.6 %collective-permute-start.16 = (bf16[2048,256]{1,0:T(8,128)(2,1)S(1)}, bf16[2048,256]{1,0:T(8,128)(2,1)S(1)}, u32[]{:S(2)}, u32[]{:S(2)}) collective-permute-start(bf16[2048,256]{1,0:T(8,128)(2,1)S(1)} %pad_maximum_fusion.8), channel_id=1, source_target_pairs={{0,1},{1,0},{2,3},{3,2},{4,5},{5,4},{6,7},{7,6},{8,9},{9,8},{10,11... | collective-permute-start | bytes 3145736 | tf_op jit(solution)/shard_map/ppermute | solution.py:34
  36.7 53.8 %collective-permute-start.17 = (bf16[2048,256]{1,0:T(8,128)(2,1)S(1)}, bf16[2048,256]{1,0:T(8,128)(2,1)}, u32[]{:S(2)}, u32[]{:S(2)}) collective-permute-start(bf16[2048,256]{1,0:T(8,128)(2,1)S(1)} %pad_maximum_fusion.8), channel_id=1, source_target_pairs={{0,2},{1,3},{2,0},{3,1},{4,6},{5,7},{6,4},{7,5},{8,10},{9,11},{10,... | collective-permute-start | bytes 3145736 | tf_op jit(solution)/shard_map/ppermute | solution.py:34
  63.5 60.8 %collective-permute-start.9 = (bf16[2048,256]{1,0:T(8,128)(2,1)S(1)}, bf16[2048,256]{1,0:T(8,128)(2,1)S(1)}, u32[]{:S(2)}, u32[]{:S(2)}) collective-permute-start(bf16[2048,256]{1,0:T(8,128)(2,1)S(1)} %pad_maximum_fusion.7), channel_id=1, source_target_pairs={{0,1},{1,0},{2,3},{3,2},{4,5},{5,4},{6,7},{7,6},{8,9},{9,8},{10,11... | collective-permute-start | bytes 3145736 | tf_op jit(solution)/shard_map/ppermute | solution.py:34
  73.8 53.6 %collective-permute-start.10 = (bf16[2048,256]{1,0:T(8,128)(2,1)S(1)}, bf16[2048,256]{1,0:T(8,128)(2,1)}, u32[]{:S(2)}, u32[]{:S(2)}) collective-permute-start(bf16[2048,256]{1,0:T(8,128)(2,1)S(1)} %pad_maximum_fusion.7), channel_id=1, source_target_pairs={{0,2},{1,3},{2,0},{3,1},{4,6},{5,7},{6,4},{7,5},{8,10},{9,11},{10,... | collective-permute-start | bytes 3145736 | tf_op jit(solution)/shard_map/ppermute | solution.py:34
  75.7 46.7 %collective-permute-start.24 = (bf16[2048,256]{1,0:T(8,128)(2,1)S(1)}, bf16[2048,256]{1,0:T(8,128)(2,1)S(1)}, u32[]{:S(2)}, u32[]{:S(2)}) collective-permute-start(bf16[2048,256]{1,0:T(8,128)(2,1)S(1)} %pad_maximum_fusion.9), channel_id=1, source_target_pairs={{0,2},{1,3},{2,0},{3,1},{4,6},{5,7},{6,4},{7,5},{8,10},{9,11},{10,... | collective-permute-start | bytes 3145736 | tf_op jit(solution)/shard_map/ppermute | solution.py:34
  86.2 57.0 %collective-permute-start.3 = (bf16[2048,256]{1,0:T(8,128)(2,1)S(1)}, bf16[2048,256]{1,0:T(8,128)(2,1)}, u32[]{:S(2)}, u32[]{:S(2)}) collective-permute-start(bf16[2048,256]{1,0:T(8,128)(2,1)S(1)} %pad_maximum_fusion.6), channel_id=1, source_target_pairs={{0,2},{1,3},{2,0},{3,1},{4,6},{5,7},{6,4},{7,5},{8,10},{9,11},{10,... | collective-permute-start | bytes 3145736 | tf_op jit(solution)/shard_map/ppermute | solution.py:34
  90.6 54.9 %collective-permute-start.2 = (bf16[2048,256]{1,0:T(8,128)(2,1)S(1)}, bf16[2048,256]{1,0:T(8,128)(2,1)S(1)}, u32[]{:S(2)}, u32[]{:S(2)}) collective-permute-start(bf16[2048,256]{1,0:T(8,128)(2,1)S(1)} %pad_maximum_fusion.6), channel_id=1, source_target_pairs={{0,1},{1,0},{2,3},{3,2},{4,5},{5,4},{6,7},{7,6},{8,9},{9,8},{10,11... | collective-permute-start | bytes 3145736 | tf_op jit(solution)/shard_map/ppermute | solution.py:34
  122.3 26.3 %collective-permute-start.23 = (bf16[2048,256]{1,0:T(8,128)(2,1)S(1)}, bf16[2048,256]{1,0:T(8,128)(2,1)S(1)}, u32[]{:S(2)}, u32[]{:S(2)}) collective-permute-start(bf16[2048,256]{1,0:T(8,128)(2,1)S(1)} %pad_maximum_fusion.9), channel_id=1, source_target_pairs={{0,1},{1,0},{2,3},{3,2},{4,5},{5,4},{6,7},{7,6},{8,9},{9,8},{10,11... | collective-permute-start | bytes 3145736 | tf_op jit(solution)/shard_map/ppermute | solution.py:34
  124.2 26.3 %collective-permute-start.25 = (bf16[2048,256]{1,0:T(8,128)(2,1)S(1)}, bf16[2048,256]{1,0:T(8,128)(2,1)S(1)}, u32[]{:S(2)}, u32[]{:S(2)}) collective-permute-start(bf16[2048,256]{1,0:T(8,128)(2,1)S(1)} %collective-permute-done.24), channel_id=1, source_target_pairs={{0,1},{1,0},{2,3},{3,2},{4,5},{5,4},{6,7},{7,6},{8,9},{9,8},{10,11... | collective-permute-start | bytes 3145736 | tf_op jit(solution)/shard_map/ppermute | solution.py:34
  127.5 51.2 %collective-permute-start.18 = (bf16[2048,256]{1,0:T(8,128)(2,1)}, bf16[2048,256]{1,0:T(8,128)(2,1)}, u32[]{:S(2)}, u32[]{:S(2)}) collective-permute-start(bf16[2048,256]{1,0:T(8,128)(2,1)} %collective-permute-done.17), channel_id=1, source_target_pairs={{0,1},{1,0},{2,3},{3,2},{4,5},{5,4},{6,7},{7,6},{8,9},{9,8},{10,11... | collective-permute-start | bytes 3145736 | tf_op jit(solution)/shard_map/ppermute | solution.py:34
  143.2 23.2 %collective-permute-start.11 = (bf16[2048,256]{1,0:T(8,128)(2,1)}, bf16[2048,256]{1,0:T(8,128)(2,1)}, u32[]{:S(2)}, u32[]{:S(2)}) collective-permute-start(bf16[2048,256]{1,0:T(8,128)(2,1)} %collective-permute-done.10), channel_id=1, source_target_pairs={{0,1},{1,0},{2,3},{3,2},{4,5},{5,4},{6,7},{7,6},{8,9},{9,8},{10,11... | collective-permute-start | bytes 3145736 | tf_op jit(solution)/shard_map/ppermute | solution.py:34
  145.4 10.1 %collective-permute-start.4 = (bf16[2048,256]{1,0:T(8,128)(2,1)}, bf16[2048,256]{1,0:T(8,128)(2,1)}, u32[]{:S(2)}, u32[]{:S(2)}) collective-permute-start(bf16[2048,256]{1,0:T(8,128)(2,1)} %collective-permute-done.3), channel_id=1, source_target_pairs={{0,1},{1,0},{2,3},{3,2},{4,5},{5,4},{6,7},{7,6},{8,9},{9,8},{10,11... | collective-permute-start | bytes 3145736 | tf_op jit(solution)/shard_map/ppermute | solution.py:34
  188.2 18.9 %collective-permute-start.27 = (f16[272,384]{1,0:T(8,128)(2,1)S(1)}, f16[272,384]{1,0:T(8,128)(2,1)S(1)}, u32[]{:S(2)}, u32[]{:S(2)}) collective-permute-start(f16[272,384]{1,0:T(8,128)(2,1)S(1)} %concatenate.151), channel_id=1, source_target_pairs={{0,16},{4,20},{8,24},{12,28},{16,0},{20,4},{24,8},{28,12},{1,17},{... | collective-permute-start | bytes 626696 | tf_op jit(solution)/shard_map/ppermute | solution.py:100
  190.8 16.3 %collective-permute-start.28 = (f16[272,384]{1,0:T(8,128)(2,1)S(1)}, f16[272,384]{1,0:T(8,128)(2,1)S(1)}, u32[]{:S(2)}, u32[]{:S(2)}) collective-permute-start(f16[272,384]{1,0:T(8,128)(2,1)S(1)} %concatenate.152), channel_id=1, source_target_pairs={{0,24},{4,28},{8,16},{12,20},{16,8},{20,12},{24,0},{28,4},{1,25},{... | collective-permute-start | bytes 626696 | tf_op jit(solution)/shard_map/ppermute | solution.py:100
  192.1 29.2 %collective-permute-start.26 = (f16[272,384]{1,0:T(8,128)(2,1)S(1)}, f16[272,384]{1,0:T(8,128)(2,1)S(1)}, u32[]{:S(2)}, u32[]{:S(2)}) collective-permute-start(f16[272,384]{1,0:T(8,128)(2,1)S(1)} %concatenate.150), channel_id=1, source_target_pairs={{0,8},{4,12},{8,0},{12,4},{16,24},{20,28},{24,16},{28,20},{1,9},{5... | collective-permute-start | bytes 626696 | tf_op jit(solution)/shard_map/ppermute | solution.py:100
  192.5 40.5 %collective-permute-start.6 = (f16[272,384]{1,0:T(8,128)(2,1)S(1)}, f16[272,384]{1,0:T(8,128)(2,1)S(1)}, u32[]{:S(2)}, u32[]{:S(2)}) collective-permute-start(f16[272,384]{1,0:T(8,128)(2,1)S(1)} %concatenate.130), channel_id=1, source_target_pairs={{0,16},{4,20},{8,24},{12,28},{16,0},{20,4},{24,8},{28,12},{1,17},{... | collective-permute-start | bytes 626696 | tf_op jit(solution)/shard_map/ppermute | solution.py:100
  195.4 37.7 %collective-permute-start.7 = (f16[272,384]{1,0:T(8,128)(2,1)S(1)}, f16[272,384]{1,0:T(8,128)(2,1)S(1)}, u32[]{:S(2)}, u32[]{:S(2)}) collective-permute-start(f16[272,384]{1,0:T(8,128)(2,1)S(1)} %concatenate.131), channel_id=1, source_target_pairs={{0,24},{4,28},{8,16},{12,20},{16,8},{20,12},{24,0},{28,4},{1,25},{... | collective-permute-start | bytes 626696 | tf_op jit(solution)/shard_map/ppermute | solution.py:100
  207.1 32.3 %collective-permute-start.5 = (f16[272,384]{1,0:T(8,128)(2,1)S(1)}, f16[272,384]{1,0:T(8,128)(2,1)S(1)}, u32[]{:S(2)}, u32[]{:S(2)}) collective-permute-start(f16[272,384]{1,0:T(8,128)(2,1)S(1)} %concatenate.129), channel_id=1, source_target_pairs={{0,8},{4,12},{8,0},{12,4},{16,24},{20,28},{24,16},{28,20},{1,9},{5... | collective-permute-start | bytes 626696 | tf_op jit(solution)/shard_map/ppermute | solution.py:100
  207.1 43.9 %collective-permute-start.13 = (f16[272,384]{1,0:T(8,128)(2,1)S(1)}, f16[272,384]{1,0:T(8,128)(2,1)S(1)}, u32[]{:S(2)}, u32[]{:S(2)}) collective-permute-start(f16[272,384]{1,0:T(8,128)(2,1)S(1)} %concatenate.137), channel_id=1, source_target_pairs={{0,16},{4,20},{8,24},{12,28},{16,0},{20,4},{24,8},{28,12},{1,17},{... | collective-permute-start | bytes 626696 | tf_op jit(solution)/shard_map/ppermute | solution.py:100
  221.3 29.9 %collective-permute-start.14 = (f16[272,384]{1,0:T(8,128)(2,1)S(1)}, f16[272,384]{1,0:T(8,128)(2,1)S(1)}, u32[]{:S(2)}, u32[]{:S(2)}) collective-permute-start(f16[272,384]{1,0:T(8,128)(2,1)S(1)} %concatenate.138), channel_id=1, source_target_pairs={{0,24},{4,28},{8,16},{12,20},{16,8},{20,12},{24,0},{28,4},{1,25},{... | collective-permute-start | bytes 626696 | tf_op jit(solution)/shard_map/ppermute | solution.py:100
  233.0 19.8 %collective-permute-start.12 = (f16[272,384]{1,0:T(8,128)(2,1)S(1)}, f16[272,384]{1,0:T(8,128)(2,1)S(1)}, u32[]{:S(2)}, u32[]{:S(2)}) collective-permute-start(f16[272,384]{1,0:T(8,128)(2,1)S(1)} %concatenate.136), channel_id=1, source_target_pairs={{0,8},{4,12},{8,0},{12,4},{16,24},{20,28},{24,16},{28,20},{1,9},{5... | collective-permute-start | bytes 626696 | tf_op jit(solution)/shard_map/ppermute | solution.py:100
  233.1 26.8 %collective-permute-start.20 = (f16[272,384]{1,0:T(8,128)(2,1)S(1)}, f16[272,384]{1,0:T(8,128)(2,1)S(1)}, u32[]{:S(2)}, u32[]{:S(2)}) collective-permute-start(f16[272,384]{1,0:T(8,128)(2,1)S(1)} %concatenate.144), channel_id=1, source_target_pairs={{0,16},{4,20},{8,24},{12,28},{16,0},{20,4},{24,8},{28,12},{1,17},{... | collective-permute-start | bytes 626696 | tf_op jit(solution)/shard_map/ppermute | solution.py:100
  239.4 22.1 %collective-permute-start.21 = (f16[272,384]{1,0:T(8,128)(2,1)S(1)}, f16[272,384]{1,0:T(8,128)(2,1)S(1)}, u32[]{:S(2)}, u32[]{:S(2)}) collective-permute-start(f16[272,384]{1,0:T(8,128)(2,1)S(1)} %concatenate.145), channel_id=1, source_target_pairs={{0,24},{4,28},{8,16},{12,20},{16,8},{20,12},{24,0},{28,4},{1,25},{... | collective-permute-start | bytes 626696 | tf_op jit(solution)/shard_map/ppermute | solution.py:100
  251.0 10.6 %collective-permute-start.19 = (f16[272,384]{1,0:T(8,128)(2,1)S(1)}, f16[272,384]{1,0:T(8,128)(2,1)S(1)}, u32[]{:S(2)}, u32[]{:S(2)}) collective-permute-start(f16[272,384]{1,0:T(8,128)(2,1)S(1)} %concatenate.143), channel_id=1, source_target_pairs={{0,8},{4,12},{8,0},{12,4},{16,24},{20,28},{24,16},{28,20},{1,9},{5... | collective-permute-start | bytes 626696 | tf_op jit(solution)/shard_map/ppermute | solution.py:100
  251.2 12.3 %collective-permute-start.32 = (f32[128,384]{1,0:T(8,128)S(1)}, f32[128,384]{1,0:T(8,128)S(1)}, u32[]{:S(2)}, u32[]{:S(2)}) collective-permute-start(f32[128,384]{1,0:T(8,128)S(1)} %get-tuple-element.44), channel_id=1, source_target_pairs={{0,4},{4,0},{8,12},{12,8},{16,20},{20,16},{24,28},{28,24},{1,5},{5... | collective-permute-start | bytes 589832 | tf_op jit(solution)/shard_map/ppermute | solution.py:113
  252.8 10.7 %collective-permute-start.29 = (f32[128,384]{1,0:T(8,128)S(1)}, f32[128,384]{1,0:T(8,128)S(1)}, u32[]{:S(2)}, u32[]{:S(2)}) collective-permute-start(f32[128,384]{1,0:T(8,128)S(1)} %get-tuple-element.38), channel_id=1, source_target_pairs={{0,4},{4,0},{8,12},{12,8},{16,20},{20,16},{24,28},{28,24},{1,5},{5... | collective-permute-start | bytes 589832 | tf_op jit(solution)/shard_map/ppermute | solution.py:113
  260.0 7.8 %collective-permute-start.30 = (f32[128,384]{1,0:T(8,128)S(1)}, f32[128,384]{1,0:T(8,128)S(1)}, u32[]{:S(2)}, u32[]{:S(2)}) collective-permute-start(f32[128,384]{1,0:T(8,128)S(1)} %get-tuple-element.40), channel_id=1, source_target_pairs={{0,4},{4,0},{8,12},{12,8},{16,20},{20,16},{24,28},{28,24},{1,5},{5... | collective-permute-start | bytes 589832 | tf_op jit(solution)/shard_map/ppermute | solution.py:113
  (37 other events, 282.3 us)
